TPU v7x, 32 devices: a whole 2x2x4 slice. The times are simulated.
32 devices in a mesh: row: 8 (over z, y), col: 4 (over x, core).
Axes of the slice: x: 2, y: 2, z: 4, core: 2. Of those that a mesh axis runs over, the one named last changes fastest.
Arguments:
- features: bfloat16 [6144, 4096], P(('row', 'col')), may hold values from -6 to 6
- cotangent: bfloat16 [6144, 8192], P(('row', 'col')), may hold values from -0.078125 to 0.078125
Outputs:
- weight_grad: float32 [4096, 8192], P('row', 'col')
All inputs are finite; a program needn't handle non-finite values.
Results may differ from a plain program's by a relative error of at most 0.0003.
Values may be sent and summed in bfloat16 or wider, within the bound.
A program may use at most 256 MiB of HBM per device.

v0:
```python
import jax
import jax.numpy as jnp
from jax import lax
from jax.sharding import PartitionSpec as P


def tokens_product(left, right):
    return lax.dot_general(
        left, right, (((0,), (0,)), ((), ())), preferred_element_type=jnp.float32
    )


def local(features, cotangent):
    row_count = lax.axis_size("row")
    width_in = features.shape[1]
    local_rows = width_in // row_count
    columns = lax.all_to_all(cotangent, "col", split_axis=1, concat_axis=0, tiled=True)
    tok_local = features.shape[0]
    exchanged = lax.all_to_all(features, "row", split_axis=1, concat_axis=0, tiled=True)
    stacked = exchanged.reshape(row_count, tok_local, local_rows)
    gathered = lax.all_gather(stacked, "col", axis=1, tiled=True)
    all_tokens = gathered.reshape(-1, local_rows)
    return tokens_product(all_tokens, lax.all_gather(columns, "row", axis=0, tiled=True))


def solution(mesh):
    placed = (P(("row", "col"), None), P(("row", "col"), None))
    return jax.shard_map(
        local, mesh=mesh, in_specs=placed, out_specs=P("row", "col"), check_vma=False
    )
```

profile of v0, /device:TPU:0, one launch (start us, length us, event | category | flops | bytes accessed | tf_op | source)
XLA Modules:
  0.0 638.1 jit_solution(12834235026453697753)
XLA Ops:
  6.5 0.0 copy-start
  6.5 0.0 all-gather.3.cloned.1.call-start
  6.5 1.7 copy.14
  8.2 44.1 %all_to_all.35 = bf16[192,8,512]{2,0,1:T(8,128)(2,1)S(1)} all-to-all(bf16[192,8,512]{2,0,1:T(8,128)(2,1)S(1)} %bitcast.19), channel_id=1, replica_groups=mesh['row'=8,'col'=4] {'row'}, dimensions={1} | all-to-all | bytes 3145728 | tf_op jit(solution)/shard_map/all_to_all | solution.py:19
  52.3 2.0 copy.6
  54.3 0.0 all-gather.3.cloned.1.call-update
  54.4 0.0 all-gather.5.cloned.1.call-start
  54.4 0.0 copy-done
  54.4 0.2 copy.13
  54.7 71.0 %all_to_all.36 = bf16[192,4,2048]{2,0,1:T(8,128)(2,1)} all-to-all(bf16[192,4,2048]{2,0,1:T(8,128)(2,1)S(1)} %bitcast.16), channel_id=1, replica_groups=mesh['row'=8,'col'=4] {'col'}, dimensions={1} | all-to-all | bytes 6291456 | tf_op jit(solution)/shard_map/all_to_all | solution.py:17
  125.7 0.0 all-gather.5.cloned.1.call-update
  125.7 4.5 all-gather.3.cloned.1.call-done
  130.2 7.8 %copy.7 = bf16[8,768,512]{2,1,0:T(8,128)(2,1)} copy(bf16[8,768,512]{2,0,1:T(8,128)(2,1)} %all-gather.3.cloned.1.call-done) | data formatting | bytes 12582912 | tf_op jit(solution)/shard_map/all_gather | solution.py:21
  138.0 472.2 %all-gather.5.cloned.1.call-done = bf16[6144,2048]{1,0:T(8,128)(2,1)} async-done(((bf16[768,2048]{1,0:T(8,128)(2,1)}), bf16[6144,2048]{1,0:T(8,128)(2,1)}) %all-gather.5.cloned.1.call-update) | async-done | bytes 25165840 | tf_op jit(solution)/shard_map/all_gather | solution.py:23
  610.2 21.0 %fusion = f32[512,2048]{1,0:T(8,128)} fusion(bf16[6144,512]{1,0:T(8,128)(2,1)} %bitcast.17, bf16[6144,2048]{1,0:T(8,128)(2,1)} %all-gather.5.cloned.1.call-done), kind=kOutput, calls=%fused_computation.2 | convolution fusion | flops 12884901888 | bytes 35651584 | tf_op jit(solution)/shard_map/dot_general | solution.py:8
Async XLA Ops:
  6.5 47.9 %copy-start = (bf16[192,8192]{1,0:T(8,128)(2,1)S(1)}, bf16[192,8192]{1,0:T(8,128)(2,1)}, u32[]{:S(2)}) copy-start(bf16[192,8192]{1,0:T(8,128)(2,1)} %param.3) | copy-start | bytes 9437188
  6.5 123.6 %all-gather.3.cloned.1.call-start = ((), (), s32[]{:S(2)}) async-start(), calls=%async_computation.2 | async-start | bytes 7864320 | tf_op jit(solution)/shard_map/all_gather | solution.py:21
  54.4 555.8 %all-gather.5.cloned.1.call-start = ((), (), s32[]{:S(2)}) async-start(), calls=%async_computation.3 | async-start | bytes 28311552 | tf_op jit(solution)/shard_map/all_gather | solution.py:23
Sparse Core Ops, SparseCore 0:
  54.5 75.6 all-gather.2
  131.7 478.4 all-gather.4
where the time goes:
time: 638 us
  waiting for transfers between devices  477 us (75%)
  blocking collectives  115 us (18%)
  matrix products  21 us (3%)
  between operations  13.4 us (2%)
  local copies, waits for them, and re-layouts  11.7 us (2%)
    all_gather x1, waiting for transfers between devices, local(): lax.all_gather(columns, 'row', axis=0, tiled=True)  472 us
    all_to_all x1, blocking collectives, local(): lax.all_to_all(cotangent, 'col', split_axis=1, concat_axis=0, tiled=True)  71 us
    all_to_all x1, blocking collectives, local(): lax.all_to_all(features, 'row', split_axis=1, concat_axis=0, tiled=True)  44.1 us
    dot_general x1, matrix products, tokens_product(): lax.dot_general(left, right, (((0,), (0,)), ((), ())), preferred_element_...  21 us
  transfers between devices with their start and end apart: 2, of which 2 were waited for; matrix products, arithmetic and copies ran while one was open for 1% of the time, Pallas kernels for 0%

commit v1 on v0

--- a/solution.py
+++ b/solution.py
@@ -1,7 +1,15 @@
+import functools
+
 import jax
 import jax.numpy as jnp
 from jax import lax
+from jax.experimental import pallas as pl
+from jax.experimental.pallas import tpu as pltpu
 from jax.sharding import PartitionSpec as P
+
+MESH = pl.DeviceIdType.MESH
+CHUNK = 256
+VMEM_MOST = 60 * 1024 * 1024
 
 
 def tokens_product(left, right):
@@ -10,7 +18,7 @@
     )
 
 
-def local(features, cotangent):
+def plain(features, cotangent):
     row_count = lax.axis_size("row")
     width_in = features.shape[1]
     local_rows = width_in // row_count
@@ -23,8 +31,269 @@
     return tokens_product(all_tokens, lax.all_gather(columns, "row", axis=0, tiled=True))
 
 
+def kernel(
+    lines, cols, feat, cot, out,
+    fall, dall, ysend, yrecv, acc,
+    f_loc, d_loc, fz_s, fz_r, fx_s, fx_r, dx_s, dx_r, rz_s, lz_s, z_r, y_s, y_r, o_s,
+):
+    row = lax.axis_index("row")
+    col = lax.axis_index("col")
+    z, y = row // 2, row % 2
+    tok = feat.shape[0]
+    rows = fall.shape[1]
+    half = rows // 2
+    chunks = dall.shape[0]
+    width = chunks * CHUNK
+    plane = tok * cols
+
+    def at_z(other):
+        return {"row": other * 2 + y, "col": col}
+
+    def at_col(other):
+        return {"row": row, "col": other}
+
+    partner = {"row": z * 2 + (1 - y), "col": col}
+
+    def remote(src, dst, s, r, dev):
+        return pltpu.make_async_remote_copy(
+            src_ref=src, dst_ref=dst, send_sem=s, recv_sem=r,
+            device_id=dev, device_id_type=MESH,
+        )
+
+    barrier = pltpu.get_barrier_semaphore()
+    for d in range(1, lines):
+        pl.semaphore_signal(barrier, inc=1, device_id=at_z((z + d) % lines), device_id_type=MESH)
+    for d in range(1, cols):
+        pl.semaphore_signal(barrier, inc=1, device_id=at_col((col + d) % cols), device_id_type=MESH)
+    pl.semaphore_signal(barrier, inc=1, device_id=partner, device_id_type=MESH)
+    pl.semaphore_wait(barrier, lines + cols - 1)
+
+    def mine(zz, cc):
+        return pl.ds(pl.multiple_of((zz * cols + cc) * tok, tok), tok)
+
+    def f_cols(zz):
+        return feat.at[:, pl.ds(pl.multiple_of(zz * rows, rows), rows)]
+
+    def f_send(zz):
+        return remote(f_cols(zz), fall.at[mine(z, col)], fz_s.at[zz], fz_r.at[z], at_z(zz))
+
+    def f_recv(zz):
+        return remote(f_cols(z), fall.at[mine(zz, col)], fz_s.at[zz], fz_r.at[zz], at_z(zz))
+
+    def f_gather(zz, d):
+        to = (col + d) % cols
+        return remote(
+            fall.at[mine(zz, col)], fall.at[mine(zz, col)],
+            fx_s.at[zz, d], fx_r.at[zz, d], at_col(to),
+        )
+
+    def f_gathered(zz, d):
+        block = fall.at[mine(zz, (col + cols - d) % cols)]
+        return remote(block, block, fx_s.at[zz, d], fx_r.at[zz, d], at_col((col + d) % cols))
+
+    def d_cols(cc, j):
+        return cot.at[:, pl.ds(pl.multiple_of(cc * width + j * CHUNK, CHUNK), CHUNK)]
+
+    def d_send(j, d):
+        to = (col + d) % cols
+        return remote(
+            d_cols(to, j), dall.at[j, mine(z, col)], dx_s.at[j, d], dx_r.at[j, d], at_col(to)
+        )
+
+    def d_recv(j, d):
+        block = dall.at[j, mine(z, (col + cols - d) % cols)]
+        return remote(block, block, dx_s.at[j, d], dx_r.at[j, d], at_col((col + d) % cols))
+
+    def plane_of(j, zz):
+        return dall.at[j, pl.ds(pl.multiple_of(zz * plane, plane), plane)]
+
+    def z_right(j, zz):
+        return remote(plane_of(j, zz), plane_of(j, zz), rz_s.at[j, zz], z_r.at[j, zz], at_z((z + 1) % lines))
+
+    def z_left(j, zz):
+        return remote(plane_of(j, zz), plane_of(j, zz), lz_s.at[j, zz], z_r.at[j, zz], at_z((z + lines - 1) % lines))
+
+    f_own = pltpu.make_async_copy(f_cols(z), fall.at[mine(z, col)], f_loc)
+    f_own.start()
+    for j in range(chunks):
+        pltpu.make_async_copy(d_cols(col, j), dall.at[j, mine(z, col)], d_loc.at[j]).start()
+    for d in range(lines - 1, 0, -1):
+        for zz in (z + d, z - d):
+            @pl.when((zz >= 0) & (zz < lines))
+            def _():
+                f_send(zz).start()
+    for j in range(chunks):
+        for d in range(1, cols):
+            d_send(j, d).start()
+
+    def send_own(j):
+        pltpu.make_async_copy(d_cols(col, j), dall.at[j, mine(z, col)], d_loc.at[j]).wait()
+        for d in range(1, cols):
+            d_recv(j, d).wait_recv()
+
+        @pl.when(z < lines - 1)
+        def _():
+            z_right(j, z).start()
+
+        @pl.when(z > 0)
+        def _():
+            z_left(j, z).start()
+
+    def relay(j):
+        for d in range(1, lines):
+            @pl.when(z - d >= 0)
+            def _():
+                z_right(j, z - d).wait_recv()
+
+                @pl.when(z < lines - 1)
+                def _():
+                    z_right(j, z - d).start()
+
+            @pl.when(z + d < lines)
+            def _():
+                z_left(j, z + d).wait_recv()
+
+                @pl.when(z > 0)
+                def _():
+                    z_left(j, z + d).start()
+
+    tile = min(CHUNK, half)
+
+    def product(j, into, which):
+        @pl.loop(0, half // tile)
+        def _(m):
+            start = pl.multiple_of(which * half + m * tile, tile)
+            into[j, pl.ds(pl.multiple_of(m * tile, tile), tile), :] = tokens_product(
+                fall[:, pl.ds(start, tile)], dall[j]
+            )
+
+    def y_copy(j):
+        return remote(ysend.at[j], yrecv.at[j], y_s.at[j], y_r.at[j], partner)
+
+    def out_copy(j):
+        return pltpu.make_async_copy(acc.at[j], out.at[:, pl.ds(j * CHUNK, CHUNK)], o_s.at[j])
+
+    def multiply(j):
+        product(j, ysend, 1 - y)
+        product(j, acc, y)
+        y_copy(j).start()
+
+    def finish(j):
+        y_copy(j).wait()
+        acc[j] += yrecv[j]
+        out_copy(j).start()
+
+    ahead = min(2, chunks)
+    for j in range(ahead):
+        send_own(j)
+    f_own.wait()
+    for d in range(1, cols):
+        f_gather(z, d).start()
+    for dz in range(1, lines):
+        zz = (z + dz) % lines
+        f_recv(zz).wait_recv()
+        for d in range(1, cols):
+            f_gather(zz, d).start()
+
+    begin = min(3, chunks - 1)
+    done = 0
+    finished = 0
+    for i in range(chunks):
+        if i + ahead < chunks:
+            send_own(i + ahead)
+        relay(i)
+        if i < begin:
+            continue
+        if done == 0:
+            for zz in range(lines):
+                for d in range(1, cols):
+                    f_gathered(zz, d).wait_recv()
+        upto = min(i + 1, done + 2) if i < chunks - 1 else chunks
+        before = done
+        while done < upto:
+            multiply(done)
+            done += 1
+        while finished < before:
+            finish(finished)
+            finished += 1
+    while finished < chunks:
+        finish(finished)
+        finished += 1
+
+    for j in range(chunks):
+        out_copy(j).wait()
+        for d in range(1, cols):
+            d_send(j, d).wait_send()
+        for d in range(lines):
+            @pl.when((z - d >= 0) & (z < lines - 1))
+            def _():
+                z_right(j, z - d).wait_send()
+
+            @pl.when((z + d < lines) & (z > 0))
+            def _():
+                z_left(j, z + d).wait_send()
+    for dz in range(1, lines):
+        f_send((z + dz) % lines).wait_send()
+    for zz in range(lines):
+        for d in range(1, cols):
+            f_gather(zz, d).wait_send()
+
+
+def fused(row_count, cols, features, cotangent):
+    lines = row_count // 2
+    tok = features.shape[0]
+    rows = features.shape[1] // lines
+    width = cotangent.shape[1] // cols
+    chunks = width // CHUNK
+    tokens = tok * cols * lines
+    half = rows // 2
+    dma = pltpu.SemaphoreType.DMA
+    return pl.pallas_call(
+        functools.partial(kernel, lines, cols),
+        out_shape=jax.ShapeDtypeStruct((half, width), jnp.float32),
+        in_specs=[pl.BlockSpec(memory_space=pl.ANY)] * 2,
+        out_specs=pl.BlockSpec(memory_space=pl.ANY),
+        scratch_shapes=[
+            pltpu.VMEM((tokens, rows), jnp.bfloat16),
+            pltpu.VMEM((chunks, tokens, CHUNK), jnp.bfloat16),
+            pltpu.VMEM((chunks, half, CHUNK), jnp.float32),
+            pltpu.VMEM((chunks, half, CHUNK), jnp.float32),
+            pltpu.VMEM((chunks, half, CHUNK), jnp.float32),
+            dma(()), dma((chunks,)),
+            dma((lines,)), dma((lines,)),
+            dma((lines, cols)), dma((lines, cols)),
+            dma((chunks, cols)), dma((chunks, cols)),
+            dma((chunks, lines)), dma((chunks, lines)), dma((chunks, lines)),
+            dma((chunks,)), dma((chunks,)), dma((chunks,)),
+        ],
+        compiler_params=pltpu.CompilerParams(
+            collective_id=0, has_side_effects=True, vmem_limit_bytes=VMEM_MOST
+        ),
+    )(features, cotangent)
+
+
+def fits(row_count, cols, features, cotangent):
+    if row_count % 2 or cotangent.shape[1] % (cols * CHUNK):
+        return False
+    if features.shape[1] % (row_count * 128):
+        return False
+    lines = row_count // 2
+    tokens = features.shape[0] * cols * lines
+    rows = features.shape[1] // lines
+    width = cotangent.shape[1] // cols
+    held = 2 * tokens * (rows + width) + 6 * rows * width
+    return lines > 1 and cols > 1 and held <= VMEM_MOST * 3 // 4
+
+
+def local(row_count, cols, features, cotangent):
+    if fits(row_count, cols, features, cotangent):
+        return fused(row_count, cols, features, cotangent)
+    return plain(features, cotangent)
+
+
 def solution(mesh):
     placed = (P(("row", "col"), None), P(("row", "col"), None))
+    body = functools.partial(local, mesh.shape["row"], mesh.shape["col"])
     return jax.shard_map(
-        local, mesh=mesh, in_specs=placed, out_specs=P("row", "col"), check_vma=False
+        body, mesh=mesh, in_specs=placed, out_specs=P("row", "col"), check_vma=False
     )

time: 638 us -> 267 us (0.42)
  waiting for transfers between devices: 477 us -> 0 us
  Pallas kernels: 0 us -> 262 us
  blocking collectives: 115 us -> 0 us
  matrix products: 21 us -> 0 us
  between operations: 13.4 us -> 0.01 us
  local copies, waits for them, and re-layouts: 11.7 us -> 4.7 us
    all_gather x2 -> x0, waiting for transfers between devices: 477 us -> none  [the longest x1 472 us: local(): lax.all_gather(columns, 'row', axis=0, tiled=True)]
    pallas_call x0 -> x1, Pallas kernels: none -> 262 us  [fused(): pl.pallas_call(functools.partial(kernel, lines, cols), out_shape=jax.Shap...]
    all_to_all x2 -> x0, blocking collectives: 115 us -> none  [the longest x1 71 us: local(): lax.all_to_all(cotangent, 'col', split_axis=1, concat_axis=0, tiled=True)]
    dot_general x1 -> x0, matrix products: 21 us -> none  [tokens_product(): lax.dot_general(left, right, (((0,), (0,)), ((), ())), preferred_element_...]
    all_gather x1 -> x0, local copies, waits for them, and re-layouts: 7.79 us -> none  [local(): gathered = lax.all_gather(stacked, 'col', axis=1, tiled=True)]
  transfers between devices with their start and end apart: 2 -> 0, of which waited for: 2 -> 0; matrix products, arithmetic and copies ran while one was open for 1% -> 0% of each run, Pallas kernels for 0% -> 0%
where the time goes in v1:
time: 267 us
  Pallas kernels  262 us (98%)
  local copies, waits for them, and re-layouts  4.7 us (2%)
    pallas_call x1, Pallas kernels, fused(): pl.pallas_call(functools.partial(kernel, lines, cols), out_shape=jax.Shap...  262 us

profile of v1, /device:TPU:0, one launch (start us, length us, event | category | flops | bytes accessed | tf_op | source)
XLA Modules:
  0.0 266.6 jit_solution(16991087857481426366)
XLA Ops:
  0.0 261.9 %shard_map.28 = f32[512,2048]{1,0:T(8,128)} custom-call(bf16[192,4096]{1,0:T(8,128)(2,1)} %feat.1, bf16[192,8192]{1,0:T(8,128)(2,1)} %cot.1), custom_call_target="tpu_custom_call" | custom-call | tf_op jit(solution)/shard_map/pallas_call | solution.py:251
  261.9 4.7 %copy.4 = f32[512,2048]{1,0:T(8,128)} copy(f32[512,2048]{1,0:T(8,128)} %shard_map.28) | data formatting | bytes 8388608

commit v2 on v1

v2 whole, which is shorter than its diff:
```python
import functools

import jax
import jax.numpy as jnp
from jax import lax
from jax.experimental import pallas as pl
from jax.experimental.pallas import tpu as pltpu
from jax.sharding import PartitionSpec as P

MESH = pl.DeviceIdType.MESH
CHUNK = 256
AHEAD = 3
LAG = 3
E_LAG = 2
VMEM_MOST = 60 * 1024 * 1024


def tokens_product(left, right):
    return lax.dot_general(
        left, right, (((0,), (0,)), ((), ())), preferred_element_type=jnp.float32
    )


def plain(features, cotangent):
    row_count = lax.axis_size("row")
    width_in = features.shape[1]
    local_rows = width_in // row_count
    columns = lax.all_to_all(cotangent, "col", split_axis=1, concat_axis=0, tiled=True)
    tok_local = features.shape[0]
    exchanged = lax.all_to_all(features, "row", split_axis=1, concat_axis=0, tiled=True)
    stacked = exchanged.reshape(row_count, tok_local, local_rows)
    gathered = lax.all_gather(stacked, "col", axis=1, tiled=True)
    all_tokens = gathered.reshape(-1, local_rows)
    return tokens_product(all_tokens, lax.all_gather(columns, "row", axis=0, tiled=True))


def partial_chunks(chunks):
    return tuple(j for j in range(2, chunks - 1) if j % 3 != 1)


def kernel(
    lines, cols, part, feat, cot, out,
    fall, fend, dall, ysend, yrecv, acc, esend, erecv, eacc, eland,
    f_loc, d_loc, fz_s, fz_r, f2_r, fr_s, gx_s, gx_r, gm_s, gm_r, dx_s, dx_r,
    rz_s, lz_s, z_r, y_s, y_r, ey_s, ey_r, ez_s, ez_r, o_s,
):
    row = lax.axis_index("row")
    col = lax.axis_index("col")
    z, y = row // 2, row % 2
    tok = feat.shape[0]
    rows = fall.shape[1]
    half = rows // 2
    chunks = dall.shape[0]
    width = chunks * CHUNK
    plane = tok * cols
    chips = cols // 2
    mate = col + 1 - 2 * (col % 2)
    last = lines - 1
    is_end = (z == 0) | (z == last)
    helps = (z == 1) | (z == last - 1)
    end = jnp.where(z * 2 < lines, 0, last)

    def at_z(other):
        return {"row": other * 2 + y, "col": col}

    def at_col(other):
        return {"row": row, "col": other}

    partner = {"row": z * 2 + (1 - y), "col": col}

    def remote(src, dst, s, r, dev):
        return pltpu.make_async_remote_copy(
            src_ref=src, dst_ref=dst, send_sem=s, recv_sem=r,
            device_id=dev, device_id_type=MESH,
        )

    barrier = pltpu.get_barrier_semaphore()
    for d in range(1, lines):
        pl.semaphore_signal(barrier, inc=1, device_id=at_z((z + d) % lines), device_id_type=MESH)
    for d in range(1, cols):
        pl.semaphore_signal(barrier, inc=1, device_id=at_col((col + d) % cols), device_id_type=MESH)
    pl.semaphore_signal(barrier, inc=1, device_id=partner, device_id_type=MESH)
    pl.semaphore_wait(barrier, lines + cols - 1)

    def mine(zz, cc):
        return pl.ds(pl.multiple_of((zz * cols + cc) * tok, tok), tok)

    def f_cols(zz):
        return feat.at[:, pl.ds(pl.multiple_of(zz * rows, rows), rows)]

    def f_send(zz):
        return remote(f_cols(zz), fall.at[mine(z, col)], fz_s.at[zz], fz_r.at[z], at_z(zz))

    def f_send_end(zz):
        to = jnp.where(zz == 0, 1, last - 1)
        return remote(f_cols(zz), fend.at[mine(z, col)], fz_s.at[zz], f2_r.at[z], at_z(to))

    def f_recv(zz):
        return remote(f_cols(z), fall.at[mine(zz, col)], fz_s.at[zz], fz_r.at[zz], at_z(zz))

    def f_recv_end(zz):
        return remote(f_cols(z), fend.at[mine(zz, col)], fz_s.at[zz], f2_r.at[zz], at_z(zz))

    def f_relay(zz):
        return remote(
            fend.at[mine(zz, col)], fall.at[mine(zz, col)], fr_s.at[zz], fz_r.at[zz], at_z(end)
        )

    held = (fall, fend)

    def g_send(b, zz, k):
        block = held[b].at[mine(zz, col)]
        return remote(
            block, block, gx_s.at[b, zz, k], gx_r.at[b, zz, k], at_col((col + 2 * k) % cols)
        )

    def g_recv(b, zz, k):
        block = held[b].at[mine(zz, (col + cols - 2 * k) % cols)]
        return remote(
            block, block, gx_s.at[b, zz, k], gx_r.at[b, zz, k], at_col((col + 2 * k) % cols)
        )

    def m_send(b, zz, k):
        block = held[b].at[mine(zz, (col + cols - 2 * k) % cols)]
        return remote(block, block, gm_s.at[b, zz, k], gm_r.at[b, zz, k], at_col(mate))

    def m_recv(b, zz, k):
        block = held[b].at[mine(zz, (mate + cols - 2 * k) % cols)]
        return remote(block, block, gm_s.at[b, zz, k], gm_r.at[b, zz, k], at_col(mate))

    def gather_start(b, zz):
        for k in range(1, chips):
            g_send(b, zz, k).start()
        m_send(b, zz, 0).start()

    def gather_forward(b, zz):
        for k in range(1, chips):
            g_recv(b, zz, k).wait_recv()
            m_send(b, zz, k).start()

    def gather_end(b, zz):
        for k in range(chips):
            m_recv(b, zz, k).wait_recv()

    def gather_drain(b, zz):
        for k in range(1, chips):
            g_send(b, zz, k).wait_send()
        for k in range(chips):
            m_send(b, zz, k).wait_send()

    def d_cols(cc, j):
        return cot.at[:, pl.ds(pl.multiple_of(cc * width + j * CHUNK, CHUNK), CHUNK)]

    def d_send(j, d):
        to = (col + d) % cols
        return remote(
            d_cols(to, j), dall.at[j, mine(z, col)], dx_s.at[j, d], dx_r.at[j, d], at_col(to)
        )

    def d_recv(j, d):
        block = dall.at[j, mine(z, (col + cols - d) % cols)]
        return remote(block, block, dx_s.at[j, d], dx_r.at[j, d], at_col((col + d) % cols))

    def plane_of(j, zz):
        return dall.at[j, pl.ds(pl.multiple_of(zz * plane, plane), plane)]

    def z_right(j, zz):
        return remote(plane_of(j, zz), plane_of(j, zz), rz_s.at[j, zz], z_r.at[j, zz], at_z((z + 1) % lines))

    def z_left(j, zz):
        return remote(plane_of(j, zz), plane_of(j, zz), lz_s.at[j, zz], z_r.at[j, zz], at_z((z + last) % lines))

    def most(j):
        return last - 1 if j in part else last

    def least(j):
        return 1 if j in part else 0

    f_own = pltpu.make_async_copy(f_cols(z), fall.at[mine(z, col)], f_loc.at[0])
    f_own.start()
    f_own_end = pltpu.make_async_copy(f_cols(end), fend.at[mine(z, col)], f_loc.at[1])

    @pl.when(helps)
    def _():
        f_own_end.start()

    for j in range(chunks):
        pltpu.make_async_copy(d_cols(col, j), dall.at[j, mine(z, col)], d_loc.at[j]).start()

    def by_helper(zz):
        return ((zz == 0) & (z != 1)) | ((zz == last) & (z != last - 1))

    for via in (False, True):
        for d in range(last, 0, -1):
            for zz in (z + d, z - d):
                inside = (zz >= 0) & (zz < lines)

                @pl.when(inside & by_helper(zz) if via else inside & ~by_helper(zz))
                def _():
                    (f_send_end if via else f_send)(zz).start()

    ahead = min(AHEAD, chunks)
    for j in range(ahead):
        for d in range(1, cols):
            d_send(j, d).start()
    f_own.wait()
    gather_start(0, z)

    def send_own(j):
        pltpu.make_async_copy(d_cols(col, j), dall.at[j, mine(z, col)], d_loc.at[j]).wait()
        for d in range(1, cols):
            d_recv(j, d).wait_recv()

        @pl.when(z < most(j))
        def _():
            z_right(j, z).start()

        @pl.when(z > least(j))
        def _():
            z_left(j, z).start()

    def relay(j):
        for d in range(1, lines):
            @pl.when((z - d >= 0) & (z <= most(j)))
            def _():
                z_right(j, z - d).wait_recv()

                @pl.when(z < most(j))
                def _():
                    z_right(j, z - d).start()

            @pl.when((z + d < lines) & (z >= least(j)))
            def _():
                z_left(j, z + d).wait_recv()

                @pl.when(z > least(j))
                def _():
                    z_left(j, z + d).start()

    tile = min(CHUNK, half)

    def product(left, j, into, at, which, start, length):
        span = pl.ds(pl.multiple_of(start, plane), length)

        @pl.loop(0, half // tile)
        def _(m):
            begin = pl.multiple_of(which * half + m * tile, tile)
            into[at, pl.ds(pl.multiple_of(m * tile, tile), tile), :] = tokens_product(
                left[span, pl.ds(begin, tile)], dall[j, span]
            )

    def y_copy(j):
        return remote(ysend.at[j], yrecv.at[j], y_s.at[j], y_r.at[j], partner)

    def out_copy(j):
        return pltpu.make_async_copy(acc.at[j], out.at[:, pl.ds(j * CHUNK, CHUNK)], o_s.at[j])

    def multiply(j):
        if j in part:
            @pl.when(is_end)
            def _():
                product(fall, j, ysend, j, 1 - y, z * plane, plane)
                product(fall, j, acc, j, y, z * plane, plane)

            @pl.when(~is_end)
            def _():
                product(fall, j, ysend, j, 1 - y, 0, lines * plane)
                product(fall, j, acc, j, y, 0, lines * plane)
        else:
            product(fall, j, ysend, j, 1 - y, 0, lines * plane)
            product(fall, j, acc, j, y, 0, lines * plane)
        y_copy(j).start()

    def finish(j):
        y_copy(j).wait()
        acc[j] += yrecv[j]
        if j in part:
            @pl.when(~is_end)
            def _():
                out_copy(j).start()
        else:
            out_copy(j).start()

    def e_copy(p):
        return remote(esend.at[p], erecv.at[p], ey_s.at[p], ey_r.at[p], partner)

    def e_move(p):
        return remote(eacc.at[p], eland.at[p], ez_s.at[p], ez_r.at[p], at_z(end))

    def extra(p):
        @pl.when(helps)
        def _():
            start = jnp.where(end == 0, plane, 0)
            product(fend, part[p], esend, p, 1 - y, start, last * plane)
            product(fend, part[p], eacc, p, y, start, last * plane)
            e_copy(p).start()

    def extra_finish(p):
        @pl.when(helps)
        def _():
            e_copy(p).wait()
            eacc[p] += erecv[p]
            e_move(p).start()

    for j in range(ahead):
        send_own(j)
    for dz in range(1, lines):
        zz = (z + dz) % lines

        @pl.when(~is_end)
        def _():
            f_recv(zz).wait_recv()
            gather_start(0, zz)
    for j in range(ahead, chunks):
        for d in range(1, cols):
            d_send(j, d).start()

    @pl.when(helps)
    def _():
        f_own_end.wait()
        gather_start(1, z)
        for dz in range(1, lines):
            zz = (z + dz) % lines

            @pl.when(zz != end)
            def _():
                f_recv_end(zz).wait_recv()
                f_relay(zz).start()
                gather_start(1, zz)

    @pl.when(is_end)
    def _():
        for dz in range(1, lines):
            zz = (z + dz) % lines
            f_recv(zz).wait_recv()
            gather_start(0, zz)

    finished = 0
    e_finished = 0
    for i in range(chunks):
        if i + ahead < chunks:
            send_own(i + ahead)
        relay(i)
        if i == 0:
            for zz in range(lines):
                gather_forward(0, zz)
            for zz in range(lines):
                gather_end(0, zz)
        if i == min(2, chunks - 1):
            for step in (gather_forward, gather_end):
                for zz in range(lines):
                    @pl.when(helps & (zz != end))
                    def _():
                        step(1, zz)
        if i in part:
            extra(part.index(i))
        multiply(i)
        if e_finished < len(part) and part[e_finished] + E_LAG <= i:
            extra_finish(e_finished)
            e_finished += 1
        if i >= LAG:
            finish(finished)
            finished += 1
    while e_finished < len(part):
        extra_finish(e_finished)
        e_finished += 1
    while finished < chunks:
        finish(finished)
        finished += 1
    for p, j in enumerate(part):
        @pl.when(is_end)
        def _():
            e_move(p).wait_recv()
            acc[j] += eland[p]
            out_copy(j).start()

    for j in range(chunks):
        out_copy(j).wait()
        for d in range(1, cols):
            d_send(j, d).wait_send()
        for d in range(lines):
            @pl.when((z - d >= 0) & (z < most(j)))
            def _():
                z_right(j, z - d).wait_send()

            @pl.when((z + d < lines) & (z > least(j)))
            def _():
                z_left(j, z + d).wait_send()
    for dz in range(1, lines):
        f_send((z + dz) % lines).wait_send()
    for zz in range(lines):
        gather_drain(0, zz)

        @pl.when(helps & (zz != end))
        def _():
            gather_drain(1, zz)

            @pl.when(zz != z)
            def _():
                f_relay(zz).wait_send()
    for p in range(len(part)):
        @pl.when(helps)
        def _():
            e_move(p).wait_send()


def fused(row_count, cols, features, cotangent):
    lines = row_count // 2
    tok = features.shape[0]
    rows = features.shape[1] // lines
    width = cotangent.shape[1] // cols
    chunks = width // CHUNK
    part = partial_chunks(chunks)
    tokens = tok * cols * lines
    half = rows // 2
    parts = max(len(part), 1)
    dma = pltpu.SemaphoreType.DMA
    whole = pltpu.VMEM((chunks, half, CHUNK), jnp.float32)
    some = pltpu.VMEM((parts, half, CHUNK), jnp.float32)
    return pl.pallas_call(
        functools.partial(kernel, lines, cols, part),
        out_shape=jax.ShapeDtypeStruct((half, width), jnp.float32),
        in_specs=[pl.BlockSpec(memory_space=pl.ANY)] * 2,
        out_specs=pl.BlockSpec(memory_space=pl.ANY),
        scratch_shapes=[
            pltpu.VMEM((tokens, rows), jnp.bfloat16),
            pltpu.VMEM((tokens, rows), jnp.bfloat16),
            pltpu.VMEM((chunks, tokens, CHUNK), jnp.bfloat16),
            whole, whole, whole, some, some, some, some,
            dma((2,)), dma((chunks,)),
            dma((lines,)), dma((lines,)), dma((lines,)), dma((lines,)),
            dma((2, lines, cols)), dma((2, lines, cols)),
            dma((2, lines, cols)), dma((2, lines, cols)),
            dma((chunks, cols)), dma((chunks, cols)),
            dma((chunks, lines)), dma((chunks, lines)), dma((chunks, lines)),
            dma((chunks,)), dma((chunks,)),
            dma((parts,)), dma((parts,)), dma((parts,)), dma((parts,)),
            dma((chunks,)),
        ],
        compiler_params=pltpu.CompilerParams(
            collective_id=0, has_side_effects=True, vmem_limit_bytes=VMEM_MOST
        ),
    )(features, cotangent)


def fits(row_count, cols, features, cotangent):
    if row_count % 2 or cotangent.shape[1] % (cols * CHUNK):
        return False
    if features.shape[1] % (row_count * 128):
        return False
    lines = row_count // 2
    tokens = features.shape[0] * cols * lines
    rows = features.shape[1] // lines
    width = cotangent.shape[1] // cols
    held = 2 * tokens * (2 * rows + width) + 14 * rows * width
    return lines > 3 and cols % 2 == 0 and held <= VMEM_MOST


def local(row_count, cols, features, cotangent):
    if fits(row_count, cols, features, cotangent):
        return fused(row_count, cols, features, cotangent)
    return plain(features, cotangent)


def solution(mesh):
    placed = (P(("row", "col"), None), P(("row", "col"), None))
    body = functools.partial(local, mesh.shape["row"], mesh.shape["col"])
    return jax.shard_map(
        body, mesh=mesh, in_specs=placed, out_specs=P("row", "col"), check_vma=False
    )
```

time: 267 us -> 260 us (0.974)
  Pallas kernels: 262 us -> 255 us
    pallas_call x1, Pallas kernels: 262 us -> 255 us  [fused(): pl.pallas_call(functools.partial(kernel, lines, cols, part), out_shape=ja...]
where the time goes in v2:
time: 260 us
  Pallas kernels  255 us (98%)
  local copies, waits for them, and re-layouts  4.7 us (2%)
    pallas_call x1, Pallas kernels, fused(): pl.pallas_call(functools.partial(kernel, lines, cols, part), out_shape=ja...  255 us

profile of v2, /device:TPU:0, one launch (start us, length us, event | category | flops | bytes accessed | tf_op | source)
XLA Modules:
  0.0 260.1 jit_solution(1070085956947116573)
XLA Ops:
  0.0 255.4 %shard_map.28 = f32[512,2048]{1,0:T(8,128)} custom-call(bf16[192,4096]{1,0:T(8,128)(2,1)} %feat.1, bf16[192,8192]{1,0:T(8,128)(2,1)} %cot.1), custom_call_target="tpu_custom_call" | custom-call | tf_op jit(solution)/shard_map/pallas_call | solution.py:420
  255.4 4.7 %copy.4 = f32[512,2048]{1,0:T(8,128)} copy(f32[512,2048]{1,0:T(8,128)} %shard_map.28) | data formatting | bytes 8388608

commit v3 on v2

--- a/solution.py
+++ b/solution.py
@@ -8,10 +8,10 @@
 from jax.sharding import PartitionSpec as P
 
 MESH = pl.DeviceIdType.MESH
-CHUNK = 256
-AHEAD = 3
-LAG = 3
-E_LAG = 2
+CHUNK = 512
+AHEAD = 2
+LAG = 1
+E_LAG = 1
 VMEM_MOST = 60 * 1024 * 1024
 
 

time: 260 us -> 257 us (0.988)
  Pallas kernels: 255 us -> 252 us
    pallas_call x1, Pallas kernels: 255 us -> 252 us  [fused(): pl.pallas_call(functools.partial(kernel, lines, cols, part), out_shape=ja...]
where the time goes in v3:
time: 257 us
  Pallas kernels  252 us (98%)
  local copies, waits for them, and re-layouts  4.7 us (2%)
    pallas_call x1, Pallas kernels, fused(): pl.pallas_call(functools.partial(kernel, lines, cols, part), out_shape=ja...  252 us

profile of v3, /device:TPU:0, one launch (start us, length us, event | category | flops | bytes accessed | tf_op | source)
XLA Modules:
  0.0 256.6 jit_solution(14093172978017302154)
XLA Ops:
  0.0 251.9 %shard_map.28 = f32[512,2048]{1,0:T(8,128)} custom-call(bf16[192,4096]{1,0:T(8,128)(2,1)} %feat.1, bf16[192,8192]{1,0:T(8,128)(2,1)} %cot.1), custom_call_target="tpu_custom_call" | custom-call | tf_op jit(solution)/shard_map/pallas_call | solution.py:420
  251.9 4.7 %copy.4 = f32[512,2048]{1,0:T(8,128)} copy(f32[512,2048]{1,0:T(8,128)} %shard_map.28) | data formatting | bytes 8388608
